TPU v7x, 256 devices: a whole 4x4x8 slice. The times are simulated.
256 devices in a mesh: seq: 32 (over y, z), head: 8 (over x, core).
Axes of the slice: x: 4, y: 4, z: 8, core: 2. Of those that a mesh axis runs over, the one named last changes fastest.
Arguments:
- query_rows: bfloat16 [32768, 4096], P('seq', 'head'), may hold values from -6 to 6
- key_rows: bfloat16 [32768, 4096], P('seq', 'head'), may hold values from -6 to 6
- value_rows: bfloat16 [32768, 4096], P('seq', 'head'), may hold values from -15 to 15
- block_picks: int32 [64, 32, 4], P('seq', 'head'), may hold values from -1 to 63, as said below
- out_weight: bfloat16 [4096, 4096], P(None, 'head'), may hold values from -0.09375 to 0.09375
Outputs:
- mixed: bfloat16 [32768, 4096], P('seq', 'head')
Inputs may be any that keep to these rules, and one draw needn't show every extreme that they name: `block_picks`: every entry that is not -1 names a block held by a lower index of seq than block b. Repeated entries of one row count once. Over the query blocks of one index of seq and the heads of one index of head, at most 2 entries name blocks of any one other index of seq, and every index of seq from 1 on has exactly 2 entries naming blocks of index 0.
All inputs are finite; a program needn't handle non-finite values.
Results may differ from a plain program's by a relative error of at most 0.0059.
Values may be sent and summed in bfloat16 or wider, within the bound.
No kernel may reach another device: no remote copies, remote signals or barrier semaphores. Data moves between devices by JAX's collectives and lax.ppermute only.
A program may use at most 192 MiB of HBM per device.

v0:
```python
import functools

import jax
import jax.numpy as jnp
from jax import lax
from jax.experimental import pallas as pl
from jax.experimental.pallas import tpu as pltpu
from jax.sharding import Mesh
from jax.sharding import PartitionSpec as P


LOG2E = 1.4426950408889634
CHUNK = 512
PAD = 16
TILE = 256
ORDER = (4, 3, -3, 2, -2, 1, -1)


def shift(array, axis, by):
    size = lax.axis_size(axis)
    return lax.ppermute(array, axis, [(i, (i + by) % size) for i in range(size)])


def stage_kernel(codes_ref, q_ref, *refs, first, last, scale, picks, parts):
    sources, rest = refs[: 2 * parts], list(refs[2 * parts :])
    state_in = () if first else [rest.pop(0) for _ in range(3)]
    if last:
        *outs, keys, values, sems, m_ref, l_ref, acc_ref = rest
    else:
        m_ref, l_ref, acc_ref, keys, values, sems = rest
    blocks, _, rows = acc_ref.shape

    copies = []
    for n in range(parts):
        for source, target in ((sources[2 * n], keys), (sources[2 * n + 1], values)):
            copy = pltpu.make_async_copy(source, target.at[pl.ds(n * blocks, blocks)], sems.at[len(copies)])
            copy.start()
            copies.append(copy)
    for new, old in zip((m_ref, l_ref, acc_ref), state_in):
        new[...] = old[...]

    def task(q, k, diagonal):
        for c in range(rows // CHUNK):
            cols = slice(c * CHUNK, (c + 1) * CHUNK)
            scores = lax.dot_general(
                keys[k], q_ref[q, cols, :], (((1,), (1,)), ((), ())), preferred_element_type=jnp.float32
            )
            if diagonal:
                kpos = lax.broadcasted_iota(jnp.int32, scores.shape, 0)
                qpos = lax.broadcasted_iota(jnp.int32, scores.shape, 1) + c * CHUNK
                scores = jnp.where(kpos <= qpos, scores, -jnp.inf)
            top = jnp.max(scores, axis=0, keepdims=True)
            if not diagonal:
                old = m_ref[q, :, cols]
                top = jnp.maximum(top, old)
            weights = jnp.exp2((scores - top) * (scale * LOG2E))
            total = jnp.sum(weights, axis=0, keepdims=True)
            part = lax.dot_general(
                values[k], weights.astype(jnp.bfloat16), (((0,), (0,)), ((), ())),
                preferred_element_type=jnp.float32,
            )
            m_ref[q, :, cols] = top
            if diagonal:
                l_ref[q, :, cols] = total
                acc_ref[q, :, cols] = part
            else:
                factor = jnp.exp2((old - top) * (scale * LOG2E))
                l_ref[q, :, cols] = l_ref[q, :, cols] * factor + total
                acc_ref[q, :, cols] = acc_ref[q, :, cols] * factor + part

    if first:
        copies[0].wait()
        copies[1].wait()

        @pl.loop(0, blocks)
        def _(q):
            task(q, q, True)

    for copy in copies[2 if first else 0 :]:
        copy.wait()

    @pl.loop(0, blocks * picks)
    def _(t):
        code = codes_ref[t]

        @pl.when(code >= 0)
        def _():
            task(t // picks, code, False)

    if last:

        z = codes_ref[blocks * picks]

        @pl.loop(0, blocks)
        def _(q):
            outs[0][(z - q) & (blocks - 1)] = (acc_ref[q] / l_ref[q]).T.astype(outs[0].dtype)


def attend_stage(codes, queries, sources, state, last, picks, tasks):
    blocks, rows, width = sources[0][0].shape
    first = state is None
    parts = len(sources)
    vmem, hbm = pl.BlockSpec(memory_space=pltpu.VMEM), pl.BlockSpec(memory_space=pl.ANY)
    state_shapes = (
        jax.ShapeDtypeStruct((blocks, 1, rows), jnp.float32),
        jax.ShapeDtypeStruct((blocks, 1, rows), jnp.float32),
        jax.ShapeDtypeStruct((blocks, width, rows), jnp.float32),
    )
    out_shape = (jax.ShapeDtypeStruct((blocks, rows, width), jnp.bfloat16),) if last else state_shapes
    return pl.pallas_call(
        functools.partial(stage_kernel, first=first, last=last, scale=width**-0.5, picks=picks, parts=parts),
        out_shape=out_shape,
        in_specs=[pl.BlockSpec(memory_space=pltpu.SMEM), vmem] + [hbm] * (2 * parts) + [vmem] * (0 if first else 3),
        out_specs=(vmem,) * len(out_shape),
        scratch_shapes=[
            pltpu.VMEM((parts * blocks, rows, width), jnp.bfloat16),
            pltpu.VMEM((parts * blocks, rows, width), jnp.bfloat16),
            pltpu.SemaphoreType.DMA((2 * parts,)),
        ]
        + [pltpu.VMEM(s.shape, s.dtype) for s in (state_shapes if last else ())],
        cost_estimate=pl.CostEstimate(
            flops=tasks * 16 * rows * rows * width,
            bytes_accessed=4 * parts * blocks * rows * width,
            transcendentals=tasks * rows * rows,
        ),
    )(codes, queries, *(r for pair in sources for r in pair), *(state or ()))


def pack_kernel(at_ref, raw_ref, got_ref, *refs, heads):
    outs, (pair, sems) = refs[:-2], refs[-2:]
    z, c = at_ref[0], at_ref[1]
    copies = [
        pltpu.make_async_copy(raw_ref.at[c], pair.at[0], sems.at[0]),
        pltpu.make_async_copy(got_ref, pair.at[1], sems.at[1]),
    ]
    for copy in copies:
        copy.start()
    for copy in copies:
        copy.wait()
    rows, width = outs[0].shape
    step = rows // (4 if rows % 64 == 0 else 3)

    @pl.loop(0, rows // step)
    def _(r):
        lines = pl.ds(pl.multiple_of(r * step, 16), step)
        for s, out in enumerate(outs):
            h = (z + s) & (len(outs) - 1)
            which = (h >> (heads.bit_length() - 1)) ^ c
            cols = pl.ds(pl.multiple_of((h & (heads - 1)) * width, width), width)
            out[lines, :] = pair[which, lines, cols]


def pack(at, raw, got, heads, count):
    rows, feature = got.shape
    vmem, hbm = pl.BlockSpec(memory_space=pltpu.VMEM), pl.BlockSpec(memory_space=pl.ANY)
    return pl.pallas_call(
        functools.partial(pack_kernel, heads=heads),
        out_shape=(jax.ShapeDtypeStruct((rows, feature // heads), raw.dtype),) * count,
        in_specs=[pl.BlockSpec(memory_space=pltpu.SMEM), hbm, hbm],
        out_specs=(vmem,) * count,
        scratch_shapes=[pltpu.VMEM((2, rows, feature), raw.dtype), pltpu.SemaphoreType.DMA((2,))],
        cost_estimate=pl.CostEstimate(flops=1 << 20, bytes_accessed=8 * rows * feature, transcendentals=0),
    )(at, raw, got)


def project_kernel(x_ref, *refs, plan, planes, last):
    parts, refs = len(plan), list(refs)
    sources = [refs.pop(0) for _ in range(parts)]
    weights = [refs.pop(0) for _ in range(2)]
    acc_in = refs.pop(0) if last else None
    outs, (data, held, sems) = refs[:-3], refs[-3:]
    depth, cols = held.shape[2:]
    copies = []

    def start(source, target):
        copy = pltpu.make_async_copy(source, target, sems.at[len(copies)])
        copy.start()
        copies.append(copy)

    plane_rows = weights[0].shape[0] // planes
    for p, (n, offset) in enumerate(plan):
        start(sources[p], data.at[p])
        base = ((x_ref[0] - n) & (planes - 1)) * plane_rows + offset
        for h in range(2):
            start(weights[h].at[pl.ds(pl.multiple_of(base, depth), depth)], held.at[p, h])
    for copy in copies:
        copy.wait()

    def product(p, h, at):
        return jnp.dot(data[p], held[p, h, :, at], preferred_element_type=jnp.float32)

    @pl.loop(0, cols // TILE)
    def _(t):
        at = pl.ds(pl.multiple_of(t * TILE, TILE), TILE)
        if last:
            for h in range(2):
                total = acc_in[h, :, at]
                for p in range(parts):
                    total = total + product(p, h, at)
                outs[h][:, at] = total.astype(outs[h].dtype)
        else:

            @pl.loop(0, 2)
            def _(h):
                outs[0][h, :, at] = jnp.zeros(outs[0].shape[1:2] + (TILE,), jnp.float32)

                @pl.loop(0, parts)
                def _(p):
                    outs[0][h, :, at] += product(p, h, at)


def project(x, sources, plan, weights, planes, acc):
    rows, depth = sources[0].shape
    parts, cols, last = len(plan), weights[0].shape[1], acc is not None
    vmem, hbm = pl.BlockSpec(memory_space=pltpu.VMEM), pl.BlockSpec(memory_space=pl.ANY)
    if last:
        out_shape = (jax.ShapeDtypeStruct((rows, cols), jnp.bfloat16),) * 2
    else:
        out_shape = (jax.ShapeDtypeStruct((2, rows, cols), jnp.float32),)
    return pl.pallas_call(
        functools.partial(project_kernel, plan=plan, planes=planes, last=last),
        out_shape=out_shape,
        in_specs=[pl.BlockSpec(memory_space=pltpu.SMEM)] + [hbm] * (parts + 2) + [vmem] * last,
        out_specs=(vmem,) * len(out_shape),
        scratch_shapes=[
            pltpu.VMEM((parts, rows, depth), jnp.bfloat16),
            pltpu.VMEM((parts, 2, depth, cols), jnp.bfloat16),
            pltpu.SemaphoreType.DMA((3 * parts,)),
        ],
        cost_estimate=pl.CostEstimate(
            flops=4 * parts * rows * depth * cols,
            bytes_accessed=2 * parts * depth * (rows + 2 * cols),
            transcendentals=0,
        ),
    )(x.reshape(1), *sources, *weights, *((acc,) if last else ()))


def program(query_rows, key_rows, value_rows, block_picks, out_weight):
    nz, nx = lax.axis_size("z"), lax.axis_size("x")
    y, z, x, c = (lax.axis_index(a) for a in ("y", "z", "x", "c"))
    tok_rows, feature = query_rows.shape
    blocks, heads, picks = block_picks.shape
    rows, width = tok_rows // blocks, feature // heads
    out_cols = out_weight.shape[1]

    place = jnp.stack((z, c))

    def swap(array):
        return array, shift(lax.dynamic_index_in_dim(array, 1 - c, 0, keepdims=False), "c", 1)

    def spread(pair):
        got = list(pack(place, *pair, heads, nz))
        for by in ORDER:
            got[by % nz] = shift(got[by % nz], "z", by)
        return jnp.stack(got)

    key_pair = swap(key_rows.reshape(blocks, rows, feature))
    value_pair = swap(value_rows.reshape(blocks, rows, feature))
    pick_rows = jnp.pad(block_picks.astype(jnp.bfloat16), ((0, 0), (0, 0), (0, width - picks)))
    pick_rows = jnp.pad(pick_rows.reshape(blocks, 1, feature), ((0, 0), (0, PAD - 1), (0, 0)))
    query_pair = swap(jnp.concatenate((query_rows.reshape(blocks, rows, feature), pick_rows), 1))
    weight_other = shift(out_weight, "c", 1)

    keys, values = {}, {}
    keys[0] = spread(key_pair)
    keys[1], keys[3] = shift(keys[0], "y", 1), shift(keys[0], "y", -1)
    values[0] = spread(value_pair)
    values[1], values[3] = shift(values[0], "y", 1), shift(values[0], "y", -1)
    keys[2], values[2] = shift(keys[1], "y", 1), shift(values[3], "y", -1)
    queries = spread(query_pair)

    mine = queries[:, rows, :picks].astype(jnp.int32)
    fresh = mine >= 0
    for gap in range(1, picks):
        same = mine[:, gap:] == mine[:, :-gap]
        fresh = fresh & ~jnp.pad(same, ((0, 0), (gap, 0)))
    block = jnp.maximum(mine, 0)
    code = ((z - block // blocks) & (nz - 1)) + nz * ((block & (blocks - 1)) ^ c)
    below = jnp.where(fresh, y - block // (nz * blocks), -1)
    near_code = jnp.where(below == 0, code, jnp.where(below == 1, code + 2 * nz, -1))
    near_code = jnp.where(below == 3, code + 4 * nz, near_code).reshape(-1)
    far_code = jnp.where(below == 2, code, -1).reshape(-1)

    def sources(n):
        return [(keys[n], values[n]), (shift(keys[n], "c", 1), shift(values[n], "c", 1))]

    state = attend_stage(near_code, queries, sources(0) + sources(1) + sources(3), None, False, picks, 32)
    (out,) = attend_stage(jnp.append(far_code, z), queries, sources(2), state, True, picks, 8)

    attended = lax.all_to_all(out, "z", split_axis=0, concat_axis=0, tiled=True)
    attended = jnp.transpose(attended, (1, 0, 2)).reshape(rows, nz * width)

    up, down = shift(attended, "x", 1), shift(attended, "x", -1)
    cut = nz * width // 2
    far = (shift(up[:, :cut], "x", 1), shift(down[:, cut:], "x", -1))
    weights = (out_weight, weight_other)
    (total,) = project(x, (attended, up, down), ((0, 0), (1, 0), (3, 0)), weights, nx, None)
    near, other = project(x, far, ((2, 0), (2, cut)), weights, nx, total)
    other = shift(other, "c", 1)
    mixed = lax.dynamic_update_slice(jnp.zeros((tok_rows, out_cols), near.dtype), near, (c * rows, jnp.int32(0)))
    return lax.dynamic_update_slice(mixed, other, ((1 - c) * rows, jnp.int32(0)))


def solution(mesh):
    finer = Mesh(mesh.devices.reshape(4, 8, 4, 2), ("y", "z", "x", "c"))
    seq, head = ("y", "z"), ("x", "c")
    return jax.shard_map(
        program,
        mesh=finer,
        in_specs=(
            P(seq, head),
            P(seq, head),
            P(seq, head),
            P(seq, head, None),
            P(None, head),
        ),
        out_specs=P(seq, head),
        check_vma=False,
    )
```

profile of v0, /device:TPU:31, one launch (start us, length us, event | category | flops | bytes accessed | tf_op | source)
XLA Modules:
  0.0 276.2 jit_solution(1668535056443420470)
XLA Ops:
  5.0 3.2 %shard_map.57 = (bf16[512,128]{1,0:T(8,128)(2,1)}, bf16[512,128]{1,0:T(8,128)(2,1)}, bf16[512,128]{1,0:T(8,128)(2,1)}, bf16[512,128]{1,0:T(8,128)(2,1)}, bf16[51...) custom-call(s32[2]{0:T(128)} %pad_add_fusion.at_ref, ...), custom_call_target="tpu_custom_call" | custom-call | flops 1048576 | bytes 2097152 | tf_op jit(solution)/shard_map/pallas_call | solution.py:156
  9.9 3.0 %collective-permute-start.20 = (bf16[512,128]{1,0:T(8,128)(2,1)}, bf16[512,128]{1,0:T(8,128)(2,1)S(1)}, u32[]{:S(2)}, u32[]{:S(2)}) collective-permute-start(bf16[512,128]{1,0:T(8,128)(2,1)} %get-tuple-element.52), channel_id=1, source_target_pairs={{0,16},{8,24},{16,32},{24,40},{32,48},{40,56},{48,0},{56,8},{1,17}... | collective-permute-start | bytes 393224 | tf_op jit(solution)/shard_map/ppermute | solution.py:21
  12.9 3.8 %collective-permute-start.21 = (bf16[512,128]{1,0:T(8,128)(2,1)}, bf16[512,128]{1,0:T(8,128)(2,1)S(1)}, u32[]{:S(2)}, u32[]{:S(2)}) collective-permute-start(bf16[512,128]{1,0:T(8,128)(2,1)} %get-tuple-element.53), channel_id=1, source_target_pairs={{0,24},{8,32},{16,40},{24,48},{32,56},{40,0},{48,8},{56,16},{1,25}... | collective-permute-start | bytes 393224 | tf_op jit(solution)/shard_map/ppermute | solution.py:21
  17.4 3.1 %shard_map.56 = (bf16[512,128]{1,0:T(8,128)(2,1)}, bf16[512,128]{1,0:T(8,128)(2,1)}, bf16[512,128]{1,0:T(8,128)(2,1)}, bf16[512,128]{1,0:T(8,128)(2,1)}, bf16[51...) custom-call(s32[2]{0:T(128)} %pad_add_fusion.at_ref, ...), custom_call_target="tpu_custom_call" | custom-call | flops 1048576 | bytes 2097152 | tf_op jit(solution)/shard_map/pallas_call | solution.py:156
  22.9 4.2 %collective-permute-start.23 = (bf16[512,128]{1,0:T(8,128)(2,1)}, bf16[512,128]{1,0:T(8,128)(2,1)S(1)}, u32[]{:S(2)}, u32[]{:S(2)}) collective-permute-start(bf16[512,128]{1,0:T(8,128)(2,1)} %get-tuple-element.55), channel_id=1, source_target_pairs={{0,40},{8,48},{16,56},{24,0},{32,8},{40,16},{48,24},{56,32},{1,41}... | collective-permute-start | bytes 393224 | tf_op jit(solution)/shard_map/ppermute | solution.py:21
  27.1 3.1 %shard_map.55 = (bf16[528,128]{1,0:T(8,128)(2,1)}, bf16[528,128]{1,0:T(8,128)(2,1)}, bf16[528,128]{1,0:T(8,128)(2,1)}, bf16[528,128]{1,0:T(8,128)(2,1)}, bf16[52...) custom-call(s32[2]{0:T(128)} %pad_add_fusion.at_ref, ...), custom_call_target="tpu_custom_call" | custom-call | flops 1048576 | bytes 2162688 | tf_op jit(solution)/shard_map/pallas_call | solution.py:156
  31.3 2.5 collective-permute-start.24
  37.4 2.9 %collective-permute-start.10 = (bf16[512,128]{1,0:T(8,128)(2,1)S(1)}, bf16[512,128]{1,0:T(8,128)(2,1)S(1)}, u32[]{:S(2)}, u32[]{:S(2)}) collective-permute-start(bf16[512,128]{1,0:T(8,128)(2,1)S(1)} %copy-done.30), channel_id=1, source_target_pairs={{0,16},{8,24},{16,32},{24,40},{32,48},{40,56},{48,0},{56,8},{1,17}... | collective-permute-start | bytes 393224 | tf_op jit(solution)/shard_map/ppermute | solution.py:21
  41.0 3.8 %collective-permute-start.11 = (bf16[512,128]{1,0:T(8,128)(2,1)S(1)}, bf16[512,128]{1,0:T(8,128)(2,1)S(1)}, u32[]{:S(2)}, u32[]{:S(2)}) collective-permute-start(bf16[512,128]{1,0:T(8,128)(2,1)S(1)} %copy-done.28), channel_id=1, source_target_pairs={{0,24},{8,32},{16,40},{24,48},{32,56},{40,0},{48,8},{56,16},{1,25}... | collective-permute-start | bytes 393224 | tf_op jit(solution)/shard_map/ppermute | solution.py:21
  46.3 4.3 %collective-permute-start.13 = (bf16[512,128]{1,0:T(8,128)(2,1)S(1)}, bf16[512,128]{1,0:T(8,128)(2,1)S(1)}, u32[]{:S(2)}, u32[]{:S(2)}) collective-permute-start(bf16[512,128]{1,0:T(8,128)(2,1)S(1)} %copy-done.26), channel_id=1, source_target_pairs={{0,40},{8,48},{16,56},{24,0},{32,8},{40,16},{48,24},{56,32},{1,41}... | collective-permute-start | bytes 393224 | tf_op jit(solution)/shard_map/ppermute | solution.py:21
  53.1 5.0 %collective-permute-done.11 = bf16[512,128]{1,0:T(8,128)(2,1)S(1)} collective-permute-done((bf16[512,128]{1,0:T(8,128)(2,1)S(1)}, bf16[512,128]{1,0:T(8,128)(2,1)S(1)}, u32[]{:S(2)}, u32[]{:S(2)}) %collective-permute-start.11) | collective-permute-done | bytes 131104 | tf_op jit(solution)/shard_map/ppermute | solution.py:21
  58.1 2.6 collective-permute-done.12
  63.1 6.0 %collective-permute-done.14 = bf16[512,128]{1,0:T(8,128)(2,1)S(1)} collective-permute-done((bf16[512,128]{1,0:T(8,128)(2,1)S(1)}, bf16[512,128]{1,0:T(8,128)(2,1)S(1)}, u32[]{:S(2)}, u32[]{:S(2)}) %collective-permute-start.14) | collective-permute-done | bytes 131104 | tf_op jit(solution)/shard_map/ppermute | solution.py:21
  69.8 4.8 %collective-permute-start.3 = (bf16[528,128]{1,0:T(8,128)(2,1)S(1)}, bf16[528,128]{1,0:T(8,128)(2,1)S(1)}, u32[]{:S(2)}, u32[]{:S(2)}) collective-permute-start(bf16[528,128]{1,0:T(8,128)(2,1)S(1)} %copy-done.21), channel_id=1, source_target_pairs={{0,24},{8,32},{16,40},{24,48},{32,56},{40,0},{48,8},{56,16},{1,25}... | collective-permute-start | bytes 405512 | tf_op jit(solution)/shard_map/ppermute | solution.py:21
  75.9 3.4 %collective-permute-start.5 = (bf16[528,128]{1,0:T(8,128)(2,1)S(1)}, bf16[528,128]{1,0:T(8,128)(2,1)S(1)}, u32[]{:S(2)}, u32[]{:S(2)}) collective-permute-start(bf16[528,128]{1,0:T(8,128)(2,1)S(1)} %copy-done.19), channel_id=1, source_target_pairs={{0,40},{8,48},{16,56},{24,0},{32,8},{40,16},{48,24},{56,32},{1,41}... | collective-permute-start | bytes 405512 | tf_op jit(solution)/shard_map/ppermute | solution.py:21
  79.3 2.5 collective-permute-done.3
  81.9 2.9 %collective-permute-start.6 = (bf16[528,128]{1,0:T(8,128)(2,1)S(1)}, bf16[528,128]{1,0:T(8,128)(2,1)S(1)}, u32[]{:S(2)}, u32[]{:S(2)}) collective-permute-start(bf16[528,128]{1,0:T(8,128)(2,1)S(1)} %copy-done.18), channel_id=1, source_target_pairs={{0,48},{8,56},{16,0},{24,8},{32,16},{40,24},{48,32},{56,40},{1,49}... | collective-permute-start | bytes 405512 | tf_op jit(solution)/shard_map/ppermute | solution.py:21
  84.8 5.6 %collective-permute-done.4 = bf16[528,128]{1,0:T(8,128)(2,1)S(1)} collective-permute-done((bf16[528,128]{1,0:T(8,128)(2,1)S(1)}, bf16[528,128]{1,0:T(8,128)(2,1)S(1)}, u32[]{:S(2)}, u32[]{:S(2)}) %collective-permute-start.4) | collective-permute-done | bytes 135200 | tf_op jit(solution)/shard_map/ppermute | solution.py:21
  92.2 7.1 %collective-permute-done.6 = bf16[528,128]{1,0:T(8,128)(2,1)S(1)} collective-permute-done((bf16[528,128]{1,0:T(8,128)(2,1)S(1)}, bf16[528,128]{1,0:T(8,128)(2,1)S(1)}, u32[]{:S(2)}, u32[]{:S(2)}) %collective-permute-start.6) | collective-permute-done | bytes 135200 | tf_op jit(solution)/shard_map/ppermute | solution.py:21
  102.5 9.8 %collective-permute-done.16.refs_4_ = bf16[8,512,128]{2,1,0:T(8,128)(2,1)} collective-permute-done((bf16[8,512,128]{2,1,0:T(8,128)(2,1)S(1)}, bf16[8,512,128]{2,1,0:T(8,128)(2,1)}, u32[]{:S(2)}, u32[]{:S(2)}) %collective-permute-start.16) | collective-permute-done | bytes 1048608 | tf_op jit(solution)/shard_map/ppermute | solution.py:21
  112.2 3.9 %collective-permute-start.37 = (bf16[8,512,128]{2,1,0:T(8,128)(2,1)}, bf16[8,512,128]{2,1,0:T(8,128)(2,1)}, u32[]{:S(2)}, u32[]{:S(2)}) collective-permute-start(bf16[8,512,128]{2,1,0:T(8,128)(2,1)} %copy-done.16), channel_id=1, source_target_pairs={{0,1},{1,0},{2,3},{3,2},{4,5},{5,4},{6,7},{7,6},{8,9},{9,8},{10,11... | collective-permute-start | bytes 3145736 | tf_op jit(solution)/shard_map/ppermute | solution.py:21
  116.2 8.6 %collective-permute-done.35.refs_8_ = bf16[8,512,128]{2,1,0:T(8,128)(2,1)} collective-permute-done((bf16[8,512,128]{2,1,0:T(8,128)(2,1)S(1)}, bf16[8,512,128]{2,1,0:T(8,128)(2,1)}, u32[]{:S(2)}, u32[]{:S(2)}) %collective-permute-start.35) | collective-permute-done | bytes 1048608 | tf_op jit(solution)/shard_map/ppermute | solution.py:21
  126.2 3.0 %collective-permute-start.17 = (bf16[8,512,128]{2,1,0:T(8,128)(2,1)}, bf16[8,512,128]{2,1,0:T(8,128)(2,1)}, u32[]{:S(2)}, u32[]{:S(2)}) collective-permute-start(bf16[8,512,128]{2,1,0:T(8,128)(2,1)} %collective-permute-done.16.refs_4_), channel_id=1, source_target_pairs={{0,64},{64,128},{128,192},{192,0},{1,65},{65,129},{129,193},{193,1... | collective-permute-start | bytes 3145736 | tf_op jit(solution)/shard_map/ppermute | solution.py:21
  131.3 18.2 %collective-permute-done.27.refs_1_ = bf16[8,512,128]{2,1,0:T(8,128)(2,1)} collective-permute-done((bf16[8,512,128]{2,1,0:T(8,128)(2,1)}, bf16[8,512,128]{2,1,0:T(8,128)(2,1)}, u32[]{:S(2)}, u32[]{:S(2)}) %collective-permute-start.27) | collective-permute-done | bytes 1048608 | tf_op jit(solution)/shard_map/ppermute | solution.py:21
  152.9 28.4 %shard_map.58 = (f32[8,1,512]{2,1,0:T(1,128)}, f32[8,1,512]{2,1,0:T(1,128)}, f32[8,128,512]{2,1,0:T(8,128)}) custom-call(s32[32]{0:T(128)} %reshape.35.codes_ref, bf16[8,528,128]{2,1,0:T(8,128)(2,1)} %copy-done.11, bf16[8,512,128]{2,1,0:T(8,128)(2,1)} %copy-done.13, bf16[8,512,128]{2,1,0:T(8,128)(2,1)} %bitcast_dynamic-update-slice_fusion.8.refs_1_, ...), custom_call_target="tpu_custom_call" | custom-call | flops 17179869184 | bytes 12582912 | tf_op jit(solution)/shard_map/pallas_call | solution.py:110
  181.4 9.3 %shard_map.59 = bf16[8,512,128]{2,1,0:T(8,128)(2,1)} custom-call(s32[33]{0:T(128)} %pad_add_fusion.1.codes_ref, bf16[8,528,128]{2,1,0:T(8,128)(2,1)} %copy-done.11, bf16[8,512,128]{2,1,0:T(8,128)(2,1)} %collective-permute-done.17.refs_0_, bf16[8,512,128]{2,1,0:T(8,128)(2,1)} %collective-permute-done.27.refs_1_, ...), custom_call_target="tpu_custom_call" | custom-call | flops 4294967296 | bytes 4194304 | tf_op jit(solution)/shard_map/pallas_call | solution.py:110
  190.7 33.4 %all_to_all.5 = bf16[8,512,128]{2,1,0:T(8,128)(2,1)S(1)} all-to-all(bf16[8,512,128]{2,1,0:T(8,128)(2,1)} %shard_map.59), channel_id=1, replica_groups=mesh['y'=4,'z'=8,'x'=4,'c'=2] {'z'}, dimensions={0} | all-to-all | bytes 2097152 | tf_op jit(solution)/shard_map/all_to_all | solution.py:290
  225.8 22.8 %collective-permute-done.38.refs_1_ = bf16[512,1024]{1,0:T(8,128)(2,1)S(1)} collective-permute-done((bf16[512,1024]{1,0:T(8,128)(2,1)S(1)}, bf16[512,1024]{1,0:T(8,128)(2,1)S(1)}, u32[]{:S(2)}, u32[]{:S(2)}) %collective-permute-start.38) | collective-permute-done | bytes 1048608 | tf_op jit(solution)/shard_map/ppermute | solution.py:21
  252.1 10.6 %shard_map.60.refs_4_ = f32[2,512,512]{2,1,0:T(8,128)} custom-call(s32[1]{0:T(128)} %bitcast.x_ref, bf16[512,1024]{1,0:T(8,128)(2,1)} %copy-done.1, bf16[512,1024]{1,0:T(8,128)(2,1)} %copy-done.3, bf16[512,1024]{1,0:T(8,128)(2,1)} %copy-done.4, bf16[4096,512]{1,0:T(8,128)(2,1)} %refs_2_.1, bf16[4096,512]{1,0:T(8,128)(2,1)} %collective-permute-done.42.refs_4_.refs_3_), custom_call_target="tpu_custom_call" | custom-call | flops 3221225472 | bytes 9437184 | tf_op jit(solution)/shard_map/pallas_call | solution.py:220
  262.7 2.6 collective-permute-done.41.refs_1_
  265.2 5.9 %shard_map.61 = (bf16[512,512]{1,0:T(8,128)(2,1)}, bf16[512,512]{1,0:T(8,128)(2,1)}) custom-call(s32[1]{0:T(128)} %bitcast.x_ref, bf16[512,512]{1,0:T(8,128)(2,1)} %collective-permute-done.39.refs_0_, bf16[512,512]{1,0:T(8,128)(2,1)} %collective-permute-done.41.refs_1_, bf16[4096,512]{1,0:T(8,128)(2,1)} %refs_2_.1, ...), custom_call_target="tpu_custom_call" | custom-call | flops 1073741824 | bytes 3145728 | tf_op jit(solution)/shard_map/pallas_call | solution.py:220
  271.1 2.5 collective-permute-start.43
  (180 shorter events, 42.9 us)
Async XLA Ops:
  3.7 19.1 %collective-permute-start = (bf16[528,512]{1,0:T(8,128)(2,1)S(1)}, bf16[528,512]{1,0:T(8,128)(2,1)S(1)}, u32[]{:S(2)}, u32[]{:S(2)}) collective-permute-start(bf16[528,512]{1,0:T(8,128)(2,1)S(1)} %dynamic-slice_bitcast_fusion), channel_id=1, source_target_pairs={{0,1},{1,0},{2,3},{3,2},{4,5},{5,4},{6,7},{7,6},{8,9},{9,8},{10,11... | collective-permute-start | bytes 1622024 | tf_op jit(solution)/shard_map/ppermute | solution.py:21
  8.2 23.2 %collective-permute-start.19 = (bf16[512,128]{1,0:T(8,128)(2,1)}, bf16[512,128]{1,0:T(8,128)(2,1)S(1)}, u32[]{:S(2)}, u32[]{:S(2)}) collective-permute-start(bf16[512,128]{1,0:T(8,128)(2,1)} %get-tuple-element.51), channel_id=1, source_target_pairs={{0,8},{8,16},{16,24},{24,32},{32,40},{40,48},{48,56},{56,0},{1,9},... | collective-permute-start | bytes 393224 | tf_op jit(solution)/shard_map/ppermute | solution.py:21
  9.9 24.6 %collective-permute-start.20 = (bf16[512,128]{1,0:T(8,128)(2,1)}, bf16[512,128]{1,0:T(8,128)(2,1)S(1)}, u32[]{:S(2)}, u32[]{:S(2)}) collective-permute-start(bf16[512,128]{1,0:T(8,128)(2,1)} %get-tuple-element.52), channel_id=1, source_target_pairs={{0,16},{8,24},{16,32},{24,40},{32,48},{40,56},{48,0},{56,8},{1,17}... | collective-permute-start | bytes 393224 | tf_op jit(solution)/shard_map/ppermute | solution.py:21
  12.9 23.1 %collective-permute-start.21 = (bf16[512,128]{1,0:T(8,128)(2,1)}, bf16[512,128]{1,0:T(8,128)(2,1)S(1)}, u32[]{:S(2)}, u32[]{:S(2)}) collective-permute-start(bf16[512,128]{1,0:T(8,128)(2,1)} %get-tuple-element.53), channel_id=1, source_target_pairs={{0,24},{8,32},{16,40},{24,48},{32,56},{40,0},{48,8},{56,16},{1,25}... | collective-permute-start | bytes 393224 | tf_op jit(solution)/shard_map/ppermute | solution.py:21
  16.6 20.8 %collective-permute-start.22 = (bf16[512,128]{1,0:T(8,128)(2,1)}, bf16[512,128]{1,0:T(8,128)(2,1)S(1)}, u32[]{:S(2)}, u32[]{:S(2)}) collective-permute-start(bf16[512,128]{1,0:T(8,128)(2,1)} %get-tuple-element.54), channel_id=1, source_target_pairs={{0,32},{8,40},{16,48},{24,56},{32,0},{40,8},{48,16},{56,24},{1,33}... | collective-permute-start | bytes 393224 | tf_op jit(solution)/shard_map/ppermute | solution.py:21
  22.9 18.1 %collective-permute-start.23 = (bf16[512,128]{1,0:T(8,128)(2,1)}, bf16[512,128]{1,0:T(8,128)(2,1)S(1)}, u32[]{:S(2)}, u32[]{:S(2)}) collective-permute-start(bf16[512,128]{1,0:T(8,128)(2,1)} %get-tuple-element.55), channel_id=1, source_target_pairs={{0,40},{8,48},{16,56},{24,0},{32,8},{40,16},{48,24},{56,32},{1,41}... | collective-permute-start | bytes 393224 | tf_op jit(solution)/shard_map/ppermute | solution.py:21
  35.9 15.2 %collective-permute-start.9 = (bf16[512,128]{1,0:T(8,128)(2,1)S(1)}, bf16[512,128]{1,0:T(8,128)(2,1)S(1)}, u32[]{:S(2)}, u32[]{:S(2)}) collective-permute-start(bf16[512,128]{1,0:T(8,128)(2,1)S(1)} %copy-done.32), channel_id=1, source_target_pairs={{0,8},{8,16},{16,24},{24,32},{32,40},{40,48},{48,56},{56,0},{1,9},... | collective-permute-start | bytes 393224 | tf_op jit(solution)/shard_map/ppermute | solution.py:21
  41.0 17.1 %collective-permute-start.11 = (bf16[512,128]{1,0:T(8,128)(2,1)S(1)}, bf16[512,128]{1,0:T(8,128)(2,1)S(1)}, u32[]{:S(2)}, u32[]{:S(2)}) collective-permute-start(bf16[512,128]{1,0:T(8,128)(2,1)S(1)} %copy-done.28), channel_id=1, source_target_pairs={{0,24},{8,32},{16,40},{24,48},{32,56},{40,0},{48,8},{56,16},{1,25}... | collective-permute-start | bytes 393224 | tf_op jit(solution)/shard_map/ppermute | solution.py:21
  45.5 15.2 %collective-permute-start.12 = (bf16[512,128]{1,0:T(8,128)(2,1)S(1)}, bf16[512,128]{1,0:T(8,128)(2,1)S(1)}, u32[]{:S(2)}, u32[]{:S(2)}) collective-permute-start(bf16[512,128]{1,0:T(8,128)(2,1)S(1)} %copy-done.27), channel_id=1, source_target_pairs={{0,32},{8,40},{16,48},{24,56},{32,0},{40,8},{48,16},{56,24},{1,33}... | collective-permute-start | bytes 393224 | tf_op jit(solution)/shard_map/ppermute | solution.py:21
  46.3 16.7 %collective-permute-start.13 = (bf16[512,128]{1,0:T(8,128)(2,1)S(1)}, bf16[512,128]{1,0:T(8,128)(2,1)S(1)}, u32[]{:S(2)}, u32[]{:S(2)}) collective-permute-start(bf16[512,128]{1,0:T(8,128)(2,1)S(1)} %copy-done.26), channel_id=1, source_target_pairs={{0,40},{8,48},{16,56},{24,0},{32,8},{40,16},{48,24},{56,32},{1,41}... | collective-permute-start | bytes 393224 | tf_op jit(solution)/shard_map/ppermute | solution.py:21
  51.2 17.9 %collective-permute-start.14 = (bf16[512,128]{1,0:T(8,128)(2,1)S(1)}, bf16[512,128]{1,0:T(8,128)(2,1)S(1)}, u32[]{:S(2)}, u32[]{:S(2)}) collective-permute-start(bf16[512,128]{1,0:T(8,128)(2,1)S(1)} %copy-done.25), channel_id=1, source_target_pairs={{0,48},{8,56},{16,0},{24,8},{32,16},{40,24},{48,32},{56,40},{1,49}... | collective-permute-start | bytes 393224 | tf_op jit(solution)/shard_map/ppermute | solution.py:21
  51.4 18.4 %collective-permute-start.15 = (bf16[512,128]{1,0:T(8,128)(2,1)S(1)}, bf16[512,128]{1,0:T(8,128)(2,1)S(1)}, u32[]{:S(2)}, u32[]{:S(2)}) collective-permute-start(bf16[512,128]{1,0:T(8,128)(2,1)S(1)} %copy-done.24), channel_id=1, source_target_pairs={{0,56},{8,0},{16,8},{24,16},{32,24},{40,32},{48,40},{56,48},{1,57}... | collective-permute-start | bytes 393224 | tf_op jit(solution)/shard_map/ppermute | solution.py:21
  58.1 16.5 %collective-permute-start.1 = (bf16[528,128]{1,0:T(8,128)(2,1)S(1)}, bf16[528,128]{1,0:T(8,128)(2,1)S(1)}, u32[]{:S(2)}, u32[]{:S(2)}) collective-permute-start(bf16[528,128]{1,0:T(8,128)(2,1)S(1)} %copy-done.23), channel_id=1, source_target_pairs={{0,8},{8,16},{16,24},{24,32},{32,40},{40,48},{48,56},{56,0},{1,9},... | collective-permute-start | bytes 405512 | tf_op jit(solution)/shard_map/ppermute | solution.py:21
  62.9 38.3 %collective-permute-start.32 = (bf16[8,512,128]{2,1,0:T(8,128)(2,1)}, bf16[8,512,128]{2,1,0:T(8,128)(2,1)S(1)}, u32[]{:S(2)}, u32[]{:S(2)}) collective-permute-start(bf16[8,512,128]{2,1,0:T(8,128)(2,1)} %bitcast_dynamic-update-slice_fusion.8.refs_1_), channel_id=1, source_target_pairs={{0,64},{64,128},{128,192},{192,0},{1,65},{65,129},{129,193},{193,1... | collective-permute-start | bytes 3145736 | tf_op jit(solution)/shard_map/ppermute | solution.py:21
  69.0 32.3 %collective-permute-start.26 = (bf16[8,512,128]{2,1,0:T(8,128)(2,1)}, bf16[8,512,128]{2,1,0:T(8,128)(2,1)S(1)}, u32[]{:S(2)}, u32[]{:S(2)}) collective-permute-start(bf16[8,512,128]{2,1,0:T(8,128)(2,1)} %bitcast_dynamic-update-slice_fusion.8.refs_1_), channel_id=1, source_target_pairs={{0,192},{64,0},{128,64},{192,128},{1,193},{65,1},{129,65},{193,129... | collective-permute-start | bytes 3145736 | tf_op jit(solution)/shard_map/ppermute | solution.py:21
  74.6 15.7 %collective-permute-start.4 = (bf16[528,128]{1,0:T(8,128)(2,1)S(1)}, bf16[528,128]{1,0:T(8,128)(2,1)S(1)}, u32[]{:S(2)}, u32[]{:S(2)}) collective-permute-start(bf16[528,128]{1,0:T(8,128)(2,1)S(1)} %copy-done.20), channel_id=1, source_target_pairs={{0,32},{8,40},{16,48},{24,56},{32,0},{40,8},{48,16},{56,24},{1,33}... | collective-permute-start | bytes 405512 | tf_op jit(solution)/shard_map/ppermute | solution.py:21
  81.9 17.5 %collective-permute-start.6 = (bf16[528,128]{1,0:T(8,128)(2,1)S(1)}, bf16[528,128]{1,0:T(8,128)(2,1)S(1)}, u32[]{:S(2)}, u32[]{:S(2)}) collective-permute-start(bf16[528,128]{1,0:T(8,128)(2,1)S(1)} %copy-done.18), channel_id=1, source_target_pairs={{0,48},{8,56},{16,0},{24,8},{32,16},{40,24},{48,32},{56,40},{1,49}... | collective-permute-start | bytes 405512 | tf_op jit(solution)/shard_map/ppermute | solution.py:21
  90.4 21.8 %collective-permute-start.16 = (bf16[8,512,128]{2,1,0:T(8,128)(2,1)S(1)}, bf16[8,512,128]{2,1,0:T(8,128)(2,1)}, u32[]{:S(2)}, u32[]{:S(2)}) collective-permute-start(bf16[8,512,128]{2,1,0:T(8,128)(2,1)S(1)} %bitcast_dynamic-update-slice_fusion.16.refs_0_), channel_id=1, source_target_pairs={{0,64},{64,128},{128,192},{192,0},{1,65},{65,129},{129,193},{193,1... | collective-permute-start | bytes 3145736 | tf_op jit(solution)/shard_map/ppermute | solution.py:21
  99.3 25.4 %collective-permute-start.35 = (bf16[8,512,128]{2,1,0:T(8,128)(2,1)S(1)}, bf16[8,512,128]{2,1,0:T(8,128)(2,1)}, u32[]{:S(2)}, u32[]{:S(2)}) collective-permute-start(bf16[8,512,128]{2,1,0:T(8,128)(2,1)S(1)} %bitcast_dynamic-update-slice_fusion.16.refs_0_), channel_id=1, source_target_pairs={{0,192},{64,0},{128,64},{192,128},{1,193},{65,1},{129,65},{193,129... | collective-permute-start | bytes 3145736 | tf_op jit(solution)/shard_map/ppermute | solution.py:21
  99.6 25.1 %collective-permute-start.31 = (bf16[8,512,128]{2,1,0:T(8,128)(2,1)}, bf16[8,512,128]{2,1,0:T(8,128)(2,1)}, u32[]{:S(2)}, u32[]{:S(2)}) collective-permute-start(bf16[8,512,128]{2,1,0:T(8,128)(2,1)} %bitcast_dynamic-update-slice_fusion.8.refs_1_), channel_id=1, source_target_pairs={{0,1},{1,0},{2,3},{3,2},{4,5},{5,4},{6,7},{7,6},{8,9},{9,8},{10,11... | collective-permute-start | bytes 3145736 | tf_op jit(solution)/shard_map/ppermute | solution.py:21
  101.2 25.0 %collective-permute-start.30 = (bf16[8,512,128]{2,1,0:T(8,128)(2,1)S(1)}, bf16[8,512,128]{2,1,0:T(8,128)(2,1)}, u32[]{:S(2)}, u32[]{:S(2)}) collective-permute-start(bf16[8,512,128]{2,1,0:T(8,128)(2,1)S(1)} %bitcast_dynamic-update-slice_fusion.16.refs_0_), channel_id=1, source_target_pairs={{0,1},{1,0},{2,3},{3,2},{4,5},{5,4},{6,7},{7,6},{8,9},{9,8},{10,11... | collective-permute-start | bytes 3145736 | tf_op jit(solution)/shard_map/ppermute | solution.py:21
  101.3 27.8 %collective-permute-start.34 = (bf16[8,512,128]{2,1,0:T(8,128)(2,1)S(1)}, bf16[8,512,128]{2,1,0:T(8,128)(2,1)}, u32[]{:S(2)}, u32[]{:S(2)}) collective-permute-start(bf16[8,512,128]{2,1,0:T(8,128)(2,1)S(1)} %collective-permute-done.32.refs_5_), channel_id=1, source_target_pairs={{0,1},{1,0},{2,3},{3,2},{4,5},{5,4},{6,7},{7,6},{8,9},{9,8},{10,11... | collective-permute-start | bytes 3145736 | tf_op jit(solution)/shard_map/ppermute | solution.py:21
  112.2 18.9 %collective-permute-start.37 = (bf16[8,512,128]{2,1,0:T(8,128)(2,1)}, bf16[8,512,128]{2,1,0:T(8,128)(2,1)}, u32[]{:S(2)}, u32[]{:S(2)}) collective-permute-start(bf16[8,512,128]{2,1,0:T(8,128)(2,1)} %copy-done.16), channel_id=1, source_target_pairs={{0,1},{1,0},{2,3},{3,2},{4,5},{5,4},{6,7},{7,6},{8,9},{9,8},{10,11... | collective-permute-start | bytes 3145736 | tf_op jit(solution)/shard_map/ppermute | solution.py:21
  124.8 24.8 %collective-permute-start.27 = (bf16[8,512,128]{2,1,0:T(8,128)(2,1)}, bf16[8,512,128]{2,1,0:T(8,128)(2,1)}, u32[]{:S(2)}, u32[]{:S(2)}) collective-permute-start(bf16[8,512,128]{2,1,0:T(8,128)(2,1)} %copy-done.16), channel_id=1, source_target_pairs={{0,192},{64,0},{128,64},{192,128},{1,193},{65,1},{129,65},{193,129... | collective-permute-start | bytes 3145736 | tf_op jit(solution)/shard_map/ppermute | solution.py:21
  124.8 28.1 %collective-permute-start.33 = (bf16[8,512,128]{2,1,0:T(8,128)(2,1)}, bf16[8,512,128]{2,1,0:T(8,128)(2,1)}, u32[]{:S(2)}, u32[]{:S(2)}) collective-permute-start(bf16[8,512,128]{2,1,0:T(8,128)(2,1)} %collective-permute-done.16.refs_4_), channel_id=1, source_target_pairs={{0,1},{1,0},{2,3},{3,2},{4,5},{5,4},{6,7},{7,6},{8,9},{9,8},{10,11... | collective-permute-start | bytes 3145736 | tf_op jit(solution)/shard_map/ppermute | solution.py:21
  126.2 25.7 %collective-permute-start.17 = (bf16[8,512,128]{2,1,0:T(8,128)(2,1)}, bf16[8,512,128]{2,1,0:T(8,128)(2,1)}, u32[]{:S(2)}, u32[]{:S(2)}) collective-permute-start(bf16[8,512,128]{2,1,0:T(8,128)(2,1)} %collective-permute-done.16.refs_4_), channel_id=1, source_target_pairs={{0,64},{64,128},{128,192},{192,0},{1,65},{65,129},{129,193},{193,1... | collective-permute-start | bytes 3145736 | tf_op jit(solution)/shard_map/ppermute | solution.py:21
  129.2 23.7 %collective-permute-start.36 = (bf16[8,512,128]{2,1,0:T(8,128)(2,1)}, bf16[8,512,128]{2,1,0:T(8,128)(2,1)}, u32[]{:S(2)}, u32[]{:S(2)}) collective-permute-start(bf16[8,512,128]{2,1,0:T(8,128)(2,1)} %collective-permute-done.35.refs_8_), channel_id=1, source_target_pairs={{0,1},{1,0},{2,3},{3,2},{4,5},{5,4},{6,7},{7,6},{8,9},{9,8},{10,11... | collective-permute-start | bytes 3145736 | tf_op jit(solution)/shard_map/ppermute | solution.py:21
  131.2 120.8 %collective-permute-start.42 = (bf16[4096,512]{1,0:T(8,128)(2,1)}, bf16[4096,512]{1,0:T(8,128)(2,1)}, u32[]{:S(2)}, u32[]{:S(2)}) collective-permute-start(bf16[4096,512]{1,0:T(8,128)(2,1)} %refs_2_.1), channel_id=1, source_target_pairs={{0,1},{1,0},{2,3},{3,2},{4,5},{5,4},{6,7},{7,6},{8,9},{9,8},{10,11... | collective-permute-start | bytes 12582920 | tf_op jit(solution)/shard_map/ppermute | solution.py:21
  149.6 31.8 %collective-permute-start.29 = (bf16[8,512,128]{2,1,0:T(8,128)(2,1)}, bf16[8,512,128]{2,1,0:T(8,128)(2,1)}, u32[]{:S(2)}, u32[]{:S(2)}) collective-permute-start(bf16[8,512,128]{2,1,0:T(8,128)(2,1)} %collective-permute-done.27.refs_1_), channel_id=1, source_target_pairs={{0,1},{1,0},{2,3},{3,2},{4,5},{5,4},{6,7},{7,6},{8,9},{9,8},{10,11... | collective-permute-start | bytes 3145736 | tf_op jit(solution)/shard_map/ppermute | solution.py:21
  151.9 29.4 %collective-permute-start.28 = (bf16[8,512,128]{2,1,0:T(8,128)(2,1)}, bf16[8,512,128]{2,1,0:T(8,128)(2,1)}, u32[]{:S(2)}, u32[]{:S(2)}) collective-permute-start(bf16[8,512,128]{2,1,0:T(8,128)(2,1)} %collective-permute-done.17.refs_0_), channel_id=1, source_target_pairs={{0,1},{1,0},{2,3},{3,2},{4,5},{5,4},{6,7},{7,6},{8,9},{9,8},{10,11... | collective-permute-start | bytes 3145736 | tf_op jit(solution)/shard_map/ppermute | solution.py:21
  224.3 24.4 %collective-permute-start.38 = (bf16[512,1024]{1,0:T(8,128)(2,1)S(1)}, bf16[512,1024]{1,0:T(8,128)(2,1)S(1)}, u32[]{:S(2)}, u32[]{:S(2)}) collective-permute-start(bf16[512,1024]{1,0:T(8,128)(2,1)S(1)} %copy_bitcast_fusion.refs_0_), channel_id=1, source_target_pairs={{0,2},{2,4},{4,6},{6,0},{1,3},{3,5},{5,7},{7,1},{8,10},{10,12},{12... | collective-permute-start | bytes 3145736 | tf_op jit(solution)/shard_map/ppermute | solution.py:21
  224.5 26.4 %collective-permute-start.40 = (bf16[512,1024]{1,0:T(8,128)(2,1)S(1)}, bf16[512,1024]{1,0:T(8,128)(2,1)S(1)}, u32[]{:S(2)}, u32[]{:S(2)}) collective-permute-start(bf16[512,1024]{1,0:T(8,128)(2,1)S(1)} %copy_bitcast_fusion.refs_0_), channel_id=1, source_target_pairs={{0,6},{2,0},{4,2},{6,4},{1,7},{3,1},{5,3},{7,5},{8,14},{10,8},{12,... | collective-permute-start | bytes 3145736 | tf_op jit(solution)/shard_map/ppermute | solution.py:21
  (45 other events, 743.2 us)
where the time goes:
time: 277 us; the launch traced here: 276 us
  waiting for transfers between devices  92.8 us (34%)
  starting transfers between devices  68.3 us (25%)
  Pallas kernels  63.6 us (23%)
  blocking collectives  33.4 us (12%)
  local copies, waits for them, and re-layouts  16 us (6%)
    ppermute x44, waiting for transfers between devices, shift(): lax.ppermute(array, axis, [(i, (i + by) % size) for i in range(size)])  92.8 us
    ppermute x44, starting transfers between devices, shift(): lax.ppermute(array, axis, [(i, (i + by) % size) for i in range(size)])  68.3 us
    pallas_call x2, Pallas kernels, attend_stage(): pl.pallas_call(functools.partial(stage_kernel, first=first, last=last, sc...  37.8 us
    all_to_all x1, blocking collectives, program(): attended = lax.all_to_all(out, 'z', split_axis=0, concat_axis=0, tiled=True)  33.4 us
    pallas_call x2, Pallas kernels, project(): pl.pallas_call(functools.partial(project_kernel, plan=plan, planes=planes...  16.4 us
    pallas_call x3, Pallas kernels, pack(): pl.pallas_call(functools.partial(pack_kernel, heads=heads), out_shape=(ja...  9.42 us
    unnamed x87, local copies, waits for them, and re-layouts  8.52 us
  transfers between devices with their start and end apart: 44, of which 14 were waited for; matrix products, arithmetic and copies ran while one was open for 5% of the time, Pallas kernels for 21%

commit v1 on v0

--- a/solution.py
+++ b/solution.py
@@ -126,43 +126,6 @@
     )(codes, queries, *(r for pair in sources for r in pair), *(state or ()))
 
 
-def pack_kernel(at_ref, raw_ref, got_ref, *refs, heads):
-    outs, (pair, sems) = refs[:-2], refs[-2:]
-    z, c = at_ref[0], at_ref[1]
-    copies = [
-        pltpu.make_async_copy(raw_ref.at[c], pair.at[0], sems.at[0]),
-        pltpu.make_async_copy(got_ref, pair.at[1], sems.at[1]),
-    ]
-    for copy in copies:
-        copy.start()
-    for copy in copies:
-        copy.wait()
-    rows, width = outs[0].shape
-    step = rows // (4 if rows % 64 == 0 else 3)
-
-    @pl.loop(0, rows // step)
-    def _(r):
-        lines = pl.ds(pl.multiple_of(r * step, 16), step)
-        for s, out in enumerate(outs):
-            h = (z + s) & (len(outs) - 1)
-            which = (h >> (heads.bit_length() - 1)) ^ c
-            cols = pl.ds(pl.multiple_of((h & (heads - 1)) * width, width), width)
-            out[lines, :] = pair[which, lines, cols]
-
-
-def pack(at, raw, got, heads, count):
-    rows, feature = got.shape
-    vmem, hbm = pl.BlockSpec(memory_space=pltpu.VMEM), pl.BlockSpec(memory_space=pl.ANY)
-    return pl.pallas_call(
-        functools.partial(pack_kernel, heads=heads),
-        out_shape=(jax.ShapeDtypeStruct((rows, feature // heads), raw.dtype),) * count,
-        in_specs=[pl.BlockSpec(memory_space=pltpu.SMEM), hbm, hbm],
-        out_specs=(vmem,) * count,
-        scratch_shapes=[pltpu.VMEM((2, rows, feature), raw.dtype), pltpu.SemaphoreType.DMA((2,))],
-        cost_estimate=pl.CostEstimate(flops=1 << 20, bytes_accessed=8 * rows * feature, transcendentals=0),
-    )(at, raw, got)
-
-
 def project_kernel(x_ref, *refs, plan, planes, last):
     parts, refs = len(plan), list(refs)
     sources = [refs.pop(0) for _ in range(parts)]
@@ -243,13 +206,18 @@
     rows, width = tok_rows // blocks, feature // heads
     out_cols = out_weight.shape[1]
 
-    place = jnp.stack((z, c))
-
     def swap(array):
-        return array, shift(lax.dynamic_index_in_dim(array, 1 - c, 0, keepdims=False), "c", 1)
+        own = lax.dynamic_index_in_dim(array, c, 0, keepdims=False)
+        other = shift(lax.dynamic_index_in_dim(array, 1 - c, 0, keepdims=False), "c", 1)
+        return jnp.stack((own, other))
 
     def spread(pair):
-        got = list(pack(place, *pair, heads, nz))
+        got = []
+        for s in range(nz):
+            h = (z + s) & (nz - 1)
+            which = (h >> (heads.bit_length() - 1)) ^ c
+            at = (which, jnp.int32(0), (h & (heads - 1)) * width)
+            got.append(lax.dynamic_slice(pair, at, (1, pair.shape[1], width))[0])
         for by in ORDER:
             got[by % nz] = shift(got[by % nz], "z", by)
         return jnp.stack(got)

time: 277 us -> 280 us (1.011)
  Pallas kernels: 63.6 us -> 54.2 us
  waiting for transfers between devices: 92.8 us -> 99.6 us
  other arithmetic: 1.43 us -> 4.61 us
  local copies, waits for them, and re-layouts: 16 us -> 19.1 us
    pallas_call x3 -> x0, Pallas kernels: 9.42 us -> none  [pack(): pl.pallas_call(functools.partial(pack_kernel, heads=heads), out_shape=(ja...]
    ppermute x44, waiting for transfers between devices: 92.8 us -> 99.6 us  [shift(): lax.ppermute(array, axis, [(i, (i + by) % size) for i in range(size)])]
    dynamic_slice x0 -> x3, local copies, waits for them, and re-layouts: none -> 3.9 us  [swap(): own = lax.dynamic_index_in_dim(array, c, 0, keepdims=False)]
    squeeze x3 -> x0, local copies, waits for them, and re-layouts: 2.89 us -> none  [swap(): lax.dynamic_index_in_dim(array, 1 - c, 0, keepdims=False)]
    unnamed x87 -> x42, local copies, waits for them, and re-layouts: 8.52 us -> 10.1 us
  transfers between devices with their start and end apart: 44 -> 44, of which waited for: 14 -> 15; matrix products, arithmetic and copies ran while one was open for 5% -> 7% of each run, Pallas kernels for 21% -> 17%
where the time goes in v1:
time: 280 us
  waiting for transfers between devices  99.6 us (36%)
  starting transfers between devices  66.3 us (24%)
  Pallas kernels  54.2 us (19%)
  blocking collectives  35.7 us (13%)
  local copies, waits for them, and re-layouts  19.1 us (7%)
  other arithmetic  4.61 us (2%)
    ppermute x44, waiting for transfers between devices, shift(): lax.ppermute(array, axis, [(i, (i + by) % size) for i in range(size)])  99.6 us
    ppermute x44, starting transfers between devices, shift(): lax.ppermute(array, axis, [(i, (i + by) % size) for i in range(size)])  66.3 us
    pallas_call x2, Pallas kernels, attend_stage(): pl.pallas_call(functools.partial(stage_kernel, first=first, last=last, sc...  37.7 us
    all_to_all x1, blocking collectives, program(): attended = lax.all_to_all(out, 'z', split_axis=0, concat_axis=0, tiled=True)  35.7 us
    pallas_call x2, Pallas kernels, project(): pl.pallas_call(functools.partial(project_kernel, plan=plan, planes=planes...  16.4 us
    unnamed x42, local copies, waits for them, and re-layouts  10.1 us
  transfers between devices with their start and end apart: 44, of which 15 were waited for; matrix products, arithmetic and copies ran while one was open for 7% of the time, Pallas kernels for 17%

profile of v1, /device:TPU:31, one launch (start us, length us, event | category | flops | bytes accessed | tf_op | source)
XLA Modules:
  0.0 279.9 jit_solution(12448649991604381693)
XLA Ops:
  0.0 2.1 constant_dynamic-slice_fusion
  8.9 3.0 %collective-permute-start.20 = (bf16[512,128]{1,0:T(8,128)(2,1)S(1)}, bf16[512,128]{1,0:T(8,128)(2,1)S(1)}, u32[]{:S(2)}, u32[]{:S(2)}) collective-permute-start(bf16[512,128]{1,0:T(8,128)(2,1)S(1)} %get-tuple-element.30), channel_id=1, source_target_pairs={{0,16},{8,24},{16,32},{24,40},{32,48},{40,56},{48,0},{56,8},{1,17}... | collective-permute-start | bytes 393224 | tf_op jit(solution)/shard_map/ppermute | solution.py:21
  12.1 3.8 %collective-permute-start.21 = (bf16[512,128]{1,0:T(8,128)(2,1)S(1)}, bf16[512,128]{1,0:T(8,128)(2,1)S(1)}, u32[]{:S(2)}, u32[]{:S(2)}) collective-permute-start(bf16[512,128]{1,0:T(8,128)(2,1)S(1)} %get-tuple-element.32), channel_id=1, source_target_pairs={{0,24},{8,32},{16,40},{24,48},{32,56},{40,0},{48,8},{56,16},{1,25}... | collective-permute-start | bytes 393224 | tf_op jit(solution)/shard_map/ppermute | solution.py:21
  17.6 4.4 %collective-permute-start.23 = (bf16[512,128]{1,0:T(8,128)(2,1)S(1)}, bf16[512,128]{1,0:T(8,128)(2,1)S(1)}, u32[]{:S(2)}, u32[]{:S(2)}) collective-permute-start(bf16[512,128]{1,0:T(8,128)(2,1)S(1)} %get-tuple-element.34), channel_id=1, source_target_pairs={{0,40},{8,48},{16,56},{24,0},{32,8},{40,16},{48,24},{56,32},{1,41}... | collective-permute-start | bytes 393224 | tf_op jit(solution)/shard_map/ppermute | solution.py:21
  22.6 2.5 collective-permute-start.24
  27.1 5.5 %collective-permute-done.21 = bf16[512,128]{1,0:T(8,128)(2,1)S(1)} collective-permute-done((bf16[512,128]{1,0:T(8,128)(2,1)S(1)}, bf16[512,128]{1,0:T(8,128)(2,1)S(1)}, u32[]{:S(2)}, u32[]{:S(2)}) %collective-permute-start.21) | collective-permute-done | bytes 131104 | tf_op jit(solution)/shard_map/ppermute | solution.py:21
  32.6 3.0 %collective-permute-start.9 = (bf16[512,128]{1,0:T(8,128)(2,1)S(1)}, bf16[512,128]{1,0:T(8,128)(2,1)S(1)}, u32[]{:S(2)}, u32[]{:S(2)}) collective-permute-start(bf16[512,128]{1,0:T(8,128)(2,1)S(1)} %get-tuple-element.39), channel_id=1, source_target_pairs={{0,8},{8,16},{16,24},{24,32},{32,40},{40,48},{48,56},{56,0},{1,9},... | collective-permute-start | bytes 393224 | tf_op jit(solution)/shard_map/ppermute | solution.py:21
  36.3 3.0 %collective-permute-start.10 = (bf16[512,128]{1,0:T(8,128)(2,1)S(1)}, bf16[512,128]{1,0:T(8,128)(2,1)S(1)}, u32[]{:S(2)}, u32[]{:S(2)}) collective-permute-start(bf16[512,128]{1,0:T(8,128)(2,1)S(1)} %get-tuple-element.40), channel_id=1, source_target_pairs={{0,16},{8,24},{16,32},{24,40},{32,48},{40,56},{48,0},{56,8},{1,17}... | collective-permute-start | bytes 393224 | tf_op jit(solution)/shard_map/ppermute | solution.py:21
  40.0 3.8 %collective-permute-start.11 = (bf16[512,128]{1,0:T(8,128)(2,1)S(1)}, bf16[512,128]{1,0:T(8,128)(2,1)S(1)}, u32[]{:S(2)}, u32[]{:S(2)}) collective-permute-start(bf16[512,128]{1,0:T(8,128)(2,1)S(1)} %get-tuple-element.42), channel_id=1, source_target_pairs={{0,24},{8,32},{16,40},{24,48},{32,56},{40,0},{48,8},{56,16},{1,25}... | collective-permute-start | bytes 393224 | tf_op jit(solution)/shard_map/ppermute | solution.py:21
  45.2 4.2 %collective-permute-start.13 = (bf16[512,128]{1,0:T(8,128)(2,1)S(1)}, bf16[512,128]{1,0:T(8,128)(2,1)S(1)}, u32[]{:S(2)}, u32[]{:S(2)}) collective-permute-start(bf16[512,128]{1,0:T(8,128)(2,1)S(1)} %get-tuple-element.44), channel_id=1, source_target_pairs={{0,40},{8,48},{16,56},{24,0},{32,8},{40,16},{48,24},{56,32},{1,41}... | collective-permute-start | bytes 393224 | tf_op jit(solution)/shard_map/ppermute | solution.py:21
  52.8 4.5 %collective-permute-done.11 = bf16[512,128]{1,0:T(8,128)(2,1)S(1)} collective-permute-done((bf16[512,128]{1,0:T(8,128)(2,1)S(1)}, bf16[512,128]{1,0:T(8,128)(2,1)S(1)}, u32[]{:S(2)}, u32[]{:S(2)}) %collective-permute-start.11) | collective-permute-done | bytes 131104 | tf_op jit(solution)/shard_map/ppermute | solution.py:21
  63.0 4.4 %collective-permute-done.14 = bf16[512,128]{1,0:T(8,128)(2,1)S(1)} collective-permute-done((bf16[512,128]{1,0:T(8,128)(2,1)S(1)}, bf16[512,128]{1,0:T(8,128)(2,1)S(1)}, u32[]{:S(2)}, u32[]{:S(2)}) %collective-permute-start.14) | collective-permute-done | bytes 131104 | tf_op jit(solution)/shard_map/ppermute | solution.py:21
  69.3 4.2 %collective-permute-start.3 = (bf16[528,128]{1,0:T(8,128)(2,1)S(1)}, bf16[528,128]{1,0:T(8,128)(2,1)S(1)}, u32[]{:S(2)}, u32[]{:S(2)}) collective-permute-start(bf16[528,128]{1,0:T(8,128)(2,1)S(1)} %get-tuple-element.22), channel_id=1, source_target_pairs={{0,24},{8,32},{16,40},{24,48},{32,56},{40,0},{48,8},{56,16},{1,25}... | collective-permute-start | bytes 405512 | tf_op jit(solution)/shard_map/ppermute | solution.py:21
  74.4 4.3 %collective-permute-start.5 = (bf16[528,128]{1,0:T(8,128)(2,1)S(1)}, bf16[528,128]{1,0:T(8,128)(2,1)S(1)}, u32[]{:S(2)}, u32[]{:S(2)}) collective-permute-start(bf16[528,128]{1,0:T(8,128)(2,1)S(1)} %get-tuple-element.24), channel_id=1, source_target_pairs={{0,40},{8,48},{16,56},{24,0},{32,8},{40,16},{48,24},{56,32},{1,41}... | collective-permute-start | bytes 405512 | tf_op jit(solution)/shard_map/ppermute | solution.py:21
  78.8 5.8 %collective-permute-done.3 = bf16[528,128]{1,0:T(8,128)(2,1)S(1)} collective-permute-done((bf16[528,128]{1,0:T(8,128)(2,1)S(1)}, bf16[528,128]{1,0:T(8,128)(2,1)S(1)}, u32[]{:S(2)}, u32[]{:S(2)}) %collective-permute-start.3) | collective-permute-done | bytes 135200 | tf_op jit(solution)/shard_map/ppermute | solution.py:21
  84.6 5.1 %collective-permute-done.4 = bf16[528,128]{1,0:T(8,128)(2,1)S(1)} collective-permute-done((bf16[528,128]{1,0:T(8,128)(2,1)S(1)}, bf16[528,128]{1,0:T(8,128)(2,1)S(1)}, u32[]{:S(2)}, u32[]{:S(2)}) %collective-permute-start.4) | collective-permute-done | bytes 135200 | tf_op jit(solution)/shard_map/ppermute | solution.py:21
  89.8 3.9 %collective-permute-start.31 = (bf16[8,512,128]{2,1,0:T(8,128)(2,1)}, bf16[8,512,128]{2,1,0:T(8,128)(2,1)}, u32[]{:S(2)}, u32[]{:S(2)}) collective-permute-start(bf16[8,512,128]{2,1,0:T(8,128)(2,1)} %bitcast_dynamic-update-slice_fusion.7.refs_1_), channel_id=1, source_target_pairs={{0,1},{1,0},{2,3},{3,2},{4,5},{5,4},{6,7},{7,6},{8,9},{9,8},{10,11... | collective-permute-start | bytes 3145736 | tf_op jit(solution)/shard_map/ppermute | solution.py:21
  93.6 5.1 %collective-permute-done.6 = bf16[528,128]{1,0:T(8,128)(2,1)S(1)} collective-permute-done((bf16[528,128]{1,0:T(8,128)(2,1)S(1)}, bf16[528,128]{1,0:T(8,128)(2,1)S(1)}, u32[]{:S(2)}, u32[]{:S(2)}) %collective-permute-start.6) | collective-permute-done | bytes 135200 | tf_op jit(solution)/shard_map/ppermute | solution.py:21
  103.4 19.7 %collective-permute-done.16.refs_4_ = bf16[8,512,128]{2,1,0:T(8,128)(2,1)} collective-permute-done((bf16[8,512,128]{2,1,0:T(8,128)(2,1)}, bf16[8,512,128]{2,1,0:T(8,128)(2,1)}, u32[]{:S(2)}, u32[]{:S(2)}) %collective-permute-start.16) | collective-permute-done | bytes 1048608 | tf_op jit(solution)/shard_map/ppermute | solution.py:21
  124.8 2.5 collective-permute-start.33
  127.3 2.3 collective-permute-start.17
  131.6 16.0 %collective-permute-done.27.refs_1_ = bf16[8,512,128]{2,1,0:T(8,128)(2,1)S(1)} collective-permute-done((bf16[8,512,128]{2,1,0:T(8,128)(2,1)}, bf16[8,512,128]{2,1,0:T(8,128)(2,1)S(1)}, u32[]{:S(2)}, u32[]{:S(2)}) %collective-permute-start.27) | collective-permute-done | bytes 1048608 | tf_op jit(solution)/shard_map/ppermute | solution.py:21
  147.6 2.4 collective-permute-start.29
  150.0 2.4 collective-permute-done.17.refs_0_
  153.3 28.4 %shard_map.55 = (f32[8,1,512]{2,1,0:T(1,128)}, f32[8,1,512]{2,1,0:T(1,128)}, f32[8,128,512]{2,1,0:T(8,128)}) custom-call(s32[32]{0:T(128)} %reshape.38.codes_ref, bf16[8,528,128]{2,1,0:T(8,128)(2,1)} %copy-done.6, bf16[8,512,128]{2,1,0:T(8,128)(2,1)} %bitcast_dynamic-update-slice_fusion.14.refs_0_, ...), custom_call_target="tpu_custom_call" | custom-call | flops 17179869184 | bytes 12582912 | tf_op jit(solution)/shard_map/pallas_call | solution.py:110
  182.8 9.3 %shard_map.56 = bf16[8,512,128]{2,1,0:T(8,128)(2,1)} custom-call(s32[33]{0:T(128)} %pad_add_fusion.codes_ref, bf16[8,528,128]{2,1,0:T(8,128)(2,1)} %copy-done.6, bf16[8,512,128]{2,1,0:T(8,128)(2,1)} %collective-permute-done.17.refs_0_, bf16[8,512,128]{2,1,0:T(8,128)(2,1)} %copy-done.10, bf16[8,512,128]{2,1,0:T(8,128)(2,1)} %collective-permute-done.28.refs_2_, ...), custom_call_target="tpu_custom_call" | custom-call | flops 4294967296 | bytes 4194304 | tf_op jit(solution)/shard_map/pallas_call | solution.py:110
  192.1 35.7 %all_to_all.5 = bf16[8,512,128]{2,1,0:T(8,128)(2,1)S(1)} all-to-all(bf16[8,512,128]{2,1,0:T(8,128)(2,1)} %shard_map.56), channel_id=1, replica_groups=mesh['y'=4,'z'=8,'x'=4,'c'=2] {'z'}, dimensions={0} | all-to-all | bytes 2097152 | tf_op jit(solution)/shard_map/all_to_all | solution.py:258
  229.5 22.8 %collective-permute-done.38.refs_1_ = bf16[512,1024]{1,0:T(8,128)(2,1)S(1)} collective-permute-done((bf16[512,1024]{1,0:T(8,128)(2,1)S(1)}, bf16[512,1024]{1,0:T(8,128)(2,1)S(1)}, u32[]{:S(2)}, u32[]{:S(2)}) %collective-permute-start.38) | collective-permute-done | bytes 1048608 | tf_op jit(solution)/shard_map/ppermute | solution.py:21
  255.9 10.6 %shard_map.57.refs_4_ = f32[2,512,512]{2,1,0:T(8,128)} custom-call(s32[1]{0:T(128)} %bitcast.x_ref, bf16[512,1024]{1,0:T(8,128)(2,1)} %copy-done, bf16[512,1024]{1,0:T(8,128)(2,1)} %copy-done.1, bf16[512,1024]{1,0:T(8,128)(2,1)} %copy-done.2, bf16[4096,512]{1,0:T(8,128)(2,1)} %refs_2_.1, bf16[4096,512]{1,0:T(8,128)(2,1)} %collective-permute-done.42.refs_4_.refs_3_), custom_call_target="tpu_custom_call" | custom-call | flops 3221225472 | bytes 9437184 | tf_op jit(solution)/shard_map/pallas_call | solution.py:183
  266.5 2.5 collective-permute-done.41.refs_1_
  268.9 5.9 %shard_map.58 = (bf16[512,512]{1,0:T(8,128)(2,1)}, bf16[512,512]{1,0:T(8,128)(2,1)}) custom-call(s32[1]{0:T(128)} %bitcast.x_ref, bf16[512,512]{1,0:T(8,128)(2,1)} %collective-permute-done.39.refs_0_, bf16[512,512]{1,0:T(8,128)(2,1)} %collective-permute-done.41.refs_1_, bf16[4096,512]{1,0:T(8,128)(2,1)} %refs_2_.1, ...), custom_call_target="tpu_custom_call" | custom-call | flops 1073741824 | bytes 3145728 | tf_op jit(solution)/shard_map/pallas_call | solution.py:183
  274.8 2.5 collective-permute-start.43
  (137 shorter events, 43.8 us)
Async XLA Ops:
  8.9 16.8 %collective-permute-start.20 = (bf16[512,128]{1,0:T(8,128)(2,1)S(1)}, bf16[512,128]{1,0:T(8,128)(2,1)S(1)}, u32[]{:S(2)}, u32[]{:S(2)}) collective-permute-start(bf16[512,128]{1,0:T(8,128)(2,1)S(1)} %get-tuple-element.30), channel_id=1, source_target_pairs={{0,16},{8,24},{16,32},{24,40},{32,48},{40,56},{48,0},{56,8},{1,17}... | collective-permute-start | bytes 393224 | tf_op jit(solution)/shard_map/ppermute | solution.py:21
  12.1 20.5 %collective-permute-start.21 = (bf16[512,128]{1,0:T(8,128)(2,1)S(1)}, bf16[512,128]{1,0:T(8,128)(2,1)S(1)}, u32[]{:S(2)}, u32[]{:S(2)}) collective-permute-start(bf16[512,128]{1,0:T(8,128)(2,1)S(1)} %get-tuple-element.32), channel_id=1, source_target_pairs={{0,24},{8,32},{16,40},{24,48},{32,56},{40,0},{48,8},{56,16},{1,25}... | collective-permute-start | bytes 393224 | tf_op jit(solution)/shard_map/ppermute | solution.py:21
  16.0 20.3 %collective-permute-start.22 = (bf16[512,128]{1,0:T(8,128)(2,1)S(1)}, bf16[512,128]{1,0:T(8,128)(2,1)S(1)}, u32[]{:S(2)}, u32[]{:S(2)}) collective-permute-start(bf16[512,128]{1,0:T(8,128)(2,1)S(1)} %get-tuple-element.33), channel_id=1, source_target_pairs={{0,32},{8,40},{16,48},{24,56},{32,0},{40,8},{48,16},{56,24},{1,33}... | collective-permute-start | bytes 393224 | tf_op jit(solution)/shard_map/ppermute | solution.py:21
  17.6 22.4 %collective-permute-start.23 = (bf16[512,128]{1,0:T(8,128)(2,1)S(1)}, bf16[512,128]{1,0:T(8,128)(2,1)S(1)}, u32[]{:S(2)}, u32[]{:S(2)}) collective-permute-start(bf16[512,128]{1,0:T(8,128)(2,1)S(1)} %get-tuple-element.34), channel_id=1, source_target_pairs={{0,40},{8,48},{16,56},{24,0},{32,8},{40,16},{48,24},{56,32},{1,41}... | collective-permute-start | bytes 393224 | tf_op jit(solution)/shard_map/ppermute | solution.py:21
  22.6 21.9 %collective-permute-start.24 = (bf16[512,128]{1,0:T(8,128)(2,1)S(1)}, bf16[512,128]{1,0:T(8,128)(2,1)S(1)}, u32[]{:S(2)}, u32[]{:S(2)}) collective-permute-start(bf16[512,128]{1,0:T(8,128)(2,1)S(1)} %get-tuple-element.31), channel_id=1, source_target_pairs={{0,48},{8,56},{16,0},{24,8},{32,16},{40,24},{48,32},{56,40},{1,49}... | collective-permute-start | bytes 393224 | tf_op jit(solution)/shard_map/ppermute | solution.py:21
  25.7 19.5 %collective-permute-start.25 = (bf16[512,128]{1,0:T(8,128)(2,1)S(1)}, bf16[512,128]{1,0:T(8,128)(2,1)S(1)}, u32[]{:S(2)}, u32[]{:S(2)}) collective-permute-start(bf16[512,128]{1,0:T(8,128)(2,1)S(1)} %get-tuple-element.27), channel_id=1, source_target_pairs={{0,56},{8,0},{16,8},{24,16},{32,24},{40,32},{48,40},{56,48},{1,57}... | collective-permute-start | bytes 393224 | tf_op jit(solution)/shard_map/ppermute | solution.py:21
  32.6 17.4 %collective-permute-start.9 = (bf16[512,128]{1,0:T(8,128)(2,1)S(1)}, bf16[512,128]{1,0:T(8,128)(2,1)S(1)}, u32[]{:S(2)}, u32[]{:S(2)}) collective-permute-start(bf16[512,128]{1,0:T(8,128)(2,1)S(1)} %get-tuple-element.39), channel_id=1, source_target_pairs={{0,8},{8,16},{16,24},{24,32},{32,40},{40,48},{48,56},{56,0},{1,9},... | collective-permute-start | bytes 393224 | tf_op jit(solution)/shard_map/ppermute | solution.py:21
  40.0 17.3 %collective-permute-start.11 = (bf16[512,128]{1,0:T(8,128)(2,1)S(1)}, bf16[512,128]{1,0:T(8,128)(2,1)S(1)}, u32[]{:S(2)}, u32[]{:S(2)}) collective-permute-start(bf16[512,128]{1,0:T(8,128)(2,1)S(1)} %get-tuple-element.42), channel_id=1, source_target_pairs={{0,24},{8,32},{16,40},{24,48},{32,56},{40,0},{48,8},{56,16},{1,25}... | collective-permute-start | bytes 393224 | tf_op jit(solution)/shard_map/ppermute | solution.py:21
  44.5 15.4 %collective-permute-start.12 = (bf16[512,128]{1,0:T(8,128)(2,1)S(1)}, bf16[512,128]{1,0:T(8,128)(2,1)S(1)}, u32[]{:S(2)}, u32[]{:S(2)}) collective-permute-start(bf16[512,128]{1,0:T(8,128)(2,1)S(1)} %get-tuple-element.43), channel_id=1, source_target_pairs={{0,32},{8,40},{16,48},{24,56},{32,0},{40,8},{48,16},{56,24},{1,33}... | collective-permute-start | bytes 393224 | tf_op jit(solution)/shard_map/ppermute | solution.py:21
  45.2 17.1 %collective-permute-start.13 = (bf16[512,128]{1,0:T(8,128)(2,1)S(1)}, bf16[512,128]{1,0:T(8,128)(2,1)S(1)}, u32[]{:S(2)}, u32[]{:S(2)}) collective-permute-start(bf16[512,128]{1,0:T(8,128)(2,1)S(1)} %get-tuple-element.44), channel_id=1, source_target_pairs={{0,40},{8,48},{16,56},{24,0},{32,8},{40,16},{48,24},{56,32},{1,41}... | collective-permute-start | bytes 393224 | tf_op jit(solution)/shard_map/ppermute | solution.py:21
  50.0 17.4 %collective-permute-start.14 = (bf16[512,128]{1,0:T(8,128)(2,1)S(1)}, bf16[512,128]{1,0:T(8,128)(2,1)S(1)}, u32[]{:S(2)}, u32[]{:S(2)}) collective-permute-start(bf16[512,128]{1,0:T(8,128)(2,1)S(1)} %get-tuple-element.41), channel_id=1, source_target_pairs={{0,48},{8,56},{16,0},{24,8},{32,16},{40,24},{48,32},{56,40},{1,49}... | collective-permute-start | bytes 393224 | tf_op jit(solution)/shard_map/ppermute | solution.py:21
  50.7 18.6 %collective-permute-start.15 = (bf16[512,128]{1,0:T(8,128)(2,1)S(1)}, bf16[512,128]{1,0:T(8,128)(2,1)S(1)}, u32[]{:S(2)}, u32[]{:S(2)}) collective-permute-start(bf16[512,128]{1,0:T(8,128)(2,1)S(1)} %get-tuple-element.37), channel_id=1, source_target_pairs={{0,56},{8,0},{16,8},{24,16},{32,24},{40,32},{48,40},{56,48},{1,57}... | collective-permute-start | bytes 393224 | tf_op jit(solution)/shard_map/ppermute | solution.py:21
  57.3 16.8 %collective-permute-start.1 = (bf16[528,128]{1,0:T(8,128)(2,1)S(1)}, bf16[528,128]{1,0:T(8,128)(2,1)S(1)}, u32[]{:S(2)}, u32[]{:S(2)}) collective-permute-start(bf16[528,128]{1,0:T(8,128)(2,1)S(1)} %get-tuple-element.19), channel_id=1, source_target_pairs={{0,8},{8,16},{16,24},{24,32},{32,40},{40,48},{48,56},{56,0},{1,9},... | collective-permute-start | bytes 405512 | tf_op jit(solution)/shard_map/ppermute | solution.py:21
  62.3 37.9 %collective-permute-start.32 = (bf16[8,512,128]{2,1,0:T(8,128)(2,1)}, bf16[8,512,128]{2,1,0:T(8,128)(2,1)S(1)}, u32[]{:S(2)}, u32[]{:S(2)}) collective-permute-start(bf16[8,512,128]{2,1,0:T(8,128)(2,1)} %bitcast_dynamic-update-slice_fusion.7.refs_1_), channel_id=1, source_target_pairs={{0,64},{64,128},{128,192},{192,0},{1,65},{65,129},{129,193},{193,1... | collective-permute-start | bytes 3145736 | tf_op jit(solution)/shard_map/ppermute | solution.py:21
  67.4 34.6 %collective-permute-start.26 = (bf16[8,512,128]{2,1,0:T(8,128)(2,1)}, bf16[8,512,128]{2,1,0:T(8,128)(2,1)S(1)}, u32[]{:S(2)}, u32[]{:S(2)}) collective-permute-start(bf16[8,512,128]{2,1,0:T(8,128)(2,1)} %bitcast_dynamic-update-slice_fusion.7.refs_1_), channel_id=1, source_target_pairs={{0,192},{64,0},{128,64},{192,128},{1,193},{65,1},{129,65},{193,129... | collective-permute-start | bytes 3145736 | tf_op jit(solution)/shard_map/ppermute | solution.py:21
  69.3 15.3 %collective-permute-start.3 = (bf16[528,128]{1,0:T(8,128)(2,1)S(1)}, bf16[528,128]{1,0:T(8,128)(2,1)S(1)}, u32[]{:S(2)}, u32[]{:S(2)}) collective-permute-start(bf16[528,128]{1,0:T(8,128)(2,1)S(1)} %get-tuple-element.22), channel_id=1, source_target_pairs={{0,24},{8,32},{16,40},{24,48},{32,56},{40,0},{48,8},{56,16},{1,25}... | collective-permute-start | bytes 405512 | tf_op jit(solution)/shard_map/ppermute | solution.py:21
  74.2 15.6 %collective-permute-start.4 = (bf16[528,128]{1,0:T(8,128)(2,1)S(1)}, bf16[528,128]{1,0:T(8,128)(2,1)S(1)}, u32[]{:S(2)}, u32[]{:S(2)}) collective-permute-start(bf16[528,128]{1,0:T(8,128)(2,1)S(1)} %get-tuple-element.23), channel_id=1, source_target_pairs={{0,32},{8,40},{16,48},{24,56},{32,0},{40,8},{48,16},{56,24},{1,33}... | collective-permute-start | bytes 405512 | tf_op jit(solution)/shard_map/ppermute | solution.py:21
  74.4 15.3 %collective-permute-start.5 = (bf16[528,128]{1,0:T(8,128)(2,1)S(1)}, bf16[528,128]{1,0:T(8,128)(2,1)S(1)}, u32[]{:S(2)}, u32[]{:S(2)}) collective-permute-start(bf16[528,128]{1,0:T(8,128)(2,1)S(1)} %get-tuple-element.24), channel_id=1, source_target_pairs={{0,40},{8,48},{16,56},{24,0},{32,8},{40,16},{48,24},{56,32},{1,41}... | collective-permute-start | bytes 405512 | tf_op jit(solution)/shard_map/ppermute | solution.py:21
  98.7 24.3 %collective-permute-start.16 = (bf16[8,512,128]{2,1,0:T(8,128)(2,1)}, bf16[8,512,128]{2,1,0:T(8,128)(2,1)}, u32[]{:S(2)}, u32[]{:S(2)}) collective-permute-start(bf16[8,512,128]{2,1,0:T(8,128)(2,1)} %bitcast_dynamic-update-slice_fusion.14.refs_0_), channel_id=1, source_target_pairs={{0,64},{64,128},{128,192},{192,0},{1,65},{65,129},{129,193},{193,1... | collective-permute-start | bytes 3145736 | tf_op jit(solution)/shard_map/ppermute | solution.py:21
  99.9 24.9 %collective-permute-start.35 = (bf16[8,512,128]{2,1,0:T(8,128)(2,1)}, bf16[8,512,128]{2,1,0:T(8,128)(2,1)}, u32[]{:S(2)}, u32[]{:S(2)}) collective-permute-start(bf16[8,512,128]{2,1,0:T(8,128)(2,1)} %bitcast_dynamic-update-slice_fusion.14.refs_0_), channel_id=1, source_target_pairs={{0,192},{64,0},{128,64},{192,128},{1,193},{65,1},{129,65},{193,129... | collective-permute-start | bytes 3145736 | tf_op jit(solution)/shard_map/ppermute | solution.py:21
  100.2 27.1 %collective-permute-start.30 = (bf16[8,512,128]{2,1,0:T(8,128)(2,1)}, bf16[8,512,128]{2,1,0:T(8,128)(2,1)}, u32[]{:S(2)}, u32[]{:S(2)}) collective-permute-start(bf16[8,512,128]{2,1,0:T(8,128)(2,1)} %bitcast_dynamic-update-slice_fusion.14.refs_0_), channel_id=1, source_target_pairs={{0,1},{1,0},{2,3},{3,2},{4,5},{5,4},{6,7},{7,6},{8,9},{9,8},{10,11... | collective-permute-start | bytes 3145736 | tf_op jit(solution)/shard_map/ppermute | solution.py:21
  102.0 27.7 %collective-permute-start.34 = (bf16[8,512,128]{2,1,0:T(8,128)(2,1)S(1)}, bf16[8,512,128]{2,1,0:T(8,128)(2,1)}, u32[]{:S(2)}, u32[]{:S(2)}) collective-permute-start(bf16[8,512,128]{2,1,0:T(8,128)(2,1)S(1)} %collective-permute-done.32.refs_5_), channel_id=1, source_target_pairs={{0,1},{1,0},{2,3},{3,2},{4,5},{5,4},{6,7},{7,6},{8,9},{9,8},{10,11... | collective-permute-start | bytes 3145736 | tf_op jit(solution)/shard_map/ppermute | solution.py:21
  103.0 28.4 %collective-permute-start.37 = (bf16[8,512,128]{2,1,0:T(8,128)(2,1)}, bf16[8,512,128]{2,1,0:T(8,128)(2,1)}, u32[]{:S(2)}, u32[]{:S(2)}) collective-permute-start(bf16[8,512,128]{2,1,0:T(8,128)(2,1)} %copy-done.9), channel_id=1, source_target_pairs={{0,1},{1,0},{2,3},{3,2},{4,5},{5,4},{6,7},{7,6},{8,9},{9,8},{10,11... | collective-permute-start | bytes 3145736 | tf_op jit(solution)/shard_map/ppermute | solution.py:21
  123.0 24.6 %collective-permute-start.27 = (bf16[8,512,128]{2,1,0:T(8,128)(2,1)}, bf16[8,512,128]{2,1,0:T(8,128)(2,1)S(1)}, u32[]{:S(2)}, u32[]{:S(2)}) collective-permute-start(bf16[8,512,128]{2,1,0:T(8,128)(2,1)} %copy-done.9), channel_id=1, source_target_pairs={{0,192},{64,0},{128,64},{192,128},{1,193},{65,1},{129,65},{193,129... | collective-permute-start | bytes 3145736 | tf_op jit(solution)/shard_map/ppermute | solution.py:21
  124.8 28.5 %collective-permute-start.33 = (bf16[8,512,128]{2,1,0:T(8,128)(2,1)}, bf16[8,512,128]{2,1,0:T(8,128)(2,1)}, u32[]{:S(2)}, u32[]{:S(2)}) collective-permute-start(bf16[8,512,128]{2,1,0:T(8,128)(2,1)} %collective-permute-done.16.refs_4_), channel_id=1, source_target_pairs={{0,1},{1,0},{2,3},{3,2},{4,5},{5,4},{6,7},{7,6},{8,9},{9,8},{10,11... | collective-permute-start | bytes 3145736 | tf_op jit(solution)/shard_map/ppermute | solution.py:21
  127.3 25.1 %collective-permute-start.17 = (bf16[8,512,128]{2,1,0:T(8,128)(2,1)}, bf16[8,512,128]{2,1,0:T(8,128)(2,1)}, u32[]{:S(2)}, u32[]{:S(2)}) collective-permute-start(bf16[8,512,128]{2,1,0:T(8,128)(2,1)} %collective-permute-done.16.refs_4_), channel_id=1, source_target_pairs={{0,64},{64,128},{128,192},{192,0},{1,65},{65,129},{129,193},{193,1... | collective-permute-start | bytes 3145736 | tf_op jit(solution)/shard_map/ppermute | solution.py:21
  129.6 23.7 %collective-permute-start.36 = (bf16[8,512,128]{2,1,0:T(8,128)(2,1)}, bf16[8,512,128]{2,1,0:T(8,128)(2,1)}, u32[]{:S(2)}, u32[]{:S(2)}) collective-permute-start(bf16[8,512,128]{2,1,0:T(8,128)(2,1)} %collective-permute-done.35.refs_8_), channel_id=1, source_target_pairs={{0,1},{1,0},{2,3},{3,2},{4,5},{5,4},{6,7},{7,6},{8,9},{9,8},{10,11... | collective-permute-start | bytes 3145736 | tf_op jit(solution)/shard_map/ppermute | solution.py:21
  131.4 124.2 %collective-permute-start.42 = (bf16[4096,512]{1,0:T(8,128)(2,1)}, bf16[4096,512]{1,0:T(8,128)(2,1)}, u32[]{:S(2)}, u32[]{:S(2)}) collective-permute-start(bf16[4096,512]{1,0:T(8,128)(2,1)} %refs_2_.1), channel_id=1, source_target_pairs={{0,1},{1,0},{2,3},{3,2},{4,5},{5,4},{6,7},{7,6},{8,9},{9,8},{10,11... | collective-permute-start | bytes 12582920 | tf_op jit(solution)/shard_map/ppermute | solution.py:21
  147.6 34.2 %collective-permute-start.29 = (bf16[8,512,128]{2,1,0:T(8,128)(2,1)S(1)}, bf16[8,512,128]{2,1,0:T(8,128)(2,1)S(1)}, u32[]{:S(2)}, u32[]{:S(2)}) collective-permute-start(bf16[8,512,128]{2,1,0:T(8,128)(2,1)S(1)} %collective-permute-done.27.refs_1_), channel_id=1, source_target_pairs={{0,1},{1,0},{2,3},{3,2},{4,5},{5,4},{6,7},{7,6},{8,9},{9,8},{10,11... | collective-permute-start | bytes 3145736 | tf_op jit(solution)/shard_map/ppermute | solution.py:21
  152.4 29.4 %collective-permute-start.28 = (bf16[8,512,128]{2,1,0:T(8,128)(2,1)}, bf16[8,512,128]{2,1,0:T(8,128)(2,1)}, u32[]{:S(2)}, u32[]{:S(2)}) collective-permute-start(bf16[8,512,128]{2,1,0:T(8,128)(2,1)} %collective-permute-done.17.refs_0_), channel_id=1, source_target_pairs={{0,1},{1,0},{2,3},{3,2},{4,5},{5,4},{6,7},{7,6},{8,9},{9,8},{10,11... | collective-permute-start | bytes 3145736 | tf_op jit(solution)/shard_map/ppermute | solution.py:21
  228.0 24.3 %collective-permute-start.38 = (bf16[512,1024]{1,0:T(8,128)(2,1)S(1)}, bf16[512,1024]{1,0:T(8,128)(2,1)S(1)}, u32[]{:S(2)}, u32[]{:S(2)}) collective-permute-start(bf16[512,1024]{1,0:T(8,128)(2,1)S(1)} %copy_bitcast_fusion.refs_0_), channel_id=1, source_target_pairs={{0,2},{2,4},{4,6},{6,0},{1,3},{3,5},{5,7},{7,1},{8,10},{10,12},{12... | collective-permute-start | bytes 3145736 | tf_op jit(solution)/shard_map/ppermute | solution.py:21
  228.2 26.4 %collective-permute-start.40 = (bf16[512,1024]{1,0:T(8,128)(2,1)S(1)}, bf16[512,1024]{1,0:T(8,128)(2,1)S(1)}, u32[]{:S(2)}, u32[]{:S(2)}) collective-permute-start(bf16[512,1024]{1,0:T(8,128)(2,1)S(1)} %copy_bitcast_fusion.refs_0_), channel_id=1, source_target_pairs={{0,6},{2,0},{4,2},{6,4},{1,7},{3,1},{5,3},{7,5},{8,14},{10,8},{12,... | collective-permute-start | bytes 3145736 | tf_op jit(solution)/shard_map/ppermute | solution.py:21
  (24 other events, 297.9 us)
